TPU v7x, 32 devices: a whole 2x2x4 slice. The times are simulated.
32 devices in a mesh: gx: 16 (over z, y, core), gy: 2 (over x).
Axes of the slice: x: 2, y: 2, z: 4, core: 2. Of those that a mesh axis runs over, the one named last changes fastest.
Arguments:
- prognostic_values: float32 [3, 6, 2048, 1024], P(None, None, 'gx', 'gy'), may hold values from -6 to 6
- forcing_host_values: bfloat16 [3, 6, 2048, 1024], P(None, None, 'gx', 'gy'), may hold values from -6 to 6
- strength: float32 [3, 6], replicated, may hold values from 50 to 200
- level_height: float32 [3], replicated, may hold values from 0.2 to 3
- pbl_height: float32 [2048, 1024], P('gx', 'gy'), may hold values from 0.2 to 3
Outputs:
- tendency: bfloat16 [3, 6, 2048, 1024], P(None, None, 'gx', 'gy')
- energy: float32 [3, 6], replicated
All inputs are finite; a program needn't handle non-finite values.
Results may differ from a plain program's by a relative error of at most 0.001.
Values sent between devices are 32-bit elements; how exact they have to be, the bound alone decides.
A program may use at most 64 MiB of HBM per device.

v0:
```python
import jax
import jax.numpy as jnp
from jax import lax
from jax.sharding import PartitionSpec as P

KX = 32
KY = 32
ramp_depth = 0.25


def cosine_table(total, modes, start, count):
    index = (start + jnp.arange(count)).astype(jnp.float32)
    waves = jnp.arange(modes).astype(jnp.float32)
    scales = jnp.where(waves == 0.0, jnp.sqrt(1.0 / total), jnp.sqrt(2.0 / total)).astype(
        jnp.float32
    )
    return scales[None, :] * jnp.cos(jnp.pi * (index[:, None] + 0.5) * waves[None, :] / total)


def per_device(prognostic_values, forcing_host_values, strength, level_height, pbl_height):
    rows = prognostic_values.shape[2]
    cols = prognostic_values.shape[3]
    largest_wavenumber = lax.Precision.HIGHEST
    row_table = cosine_table(rows * lax.axis_size("gx"), KX, lax.axis_index("gx") * rows, rows)
    col_table = cosine_table(cols * lax.axis_size("gy"), KY, lax.axis_index("gy") * cols, cols)
    diff = forcing_host_values.astype(jnp.float32) - prognostic_values
    part = jnp.einsum("...ij,jb->...ib", diff, col_table, precision=largest_wavenumber)
    mode_factors = lax.psum(
        jnp.einsum("ia,...ib->...ab", row_table, part, precision=largest_wavenumber), ("gx", "gy")
    )
    restored_fields = jnp.einsum(
        "ia,lvab->lvib", row_table, mode_factors, precision=largest_wavenumber
    )
    recon = jnp.einsum("lvib,jb->lvij", restored_fields, col_table, precision=largest_wavenumber)
    damping_share = 1.0 / (
        1.0 + jnp.exp(-(level_height[:, None, None] - pbl_height[None]) / ramp_depth)
    )
    tendency = (strength[:, :, None, None] * damping_share[:, None] * recon).astype(jnp.bfloat16)
    energy = jnp.sum(mode_factors * mode_factors, axis=(2, 3)) / (KX * KY)
    return (tendency, energy)


def solution(mesh):
    return jax.shard_map(
        per_device,
        mesh=mesh,
        in_specs=(P(None, None, "gx", "gy"), P(None, None, "gx", "gy"), P(), P(), P("gx", "gy")),
        out_specs=(P(None, None, "gx", "gy"), P()),
        check_vma=False,
    )
```

profile of v0, /device:TPU:8, one launch (start us, length us, event | category | flops | bytes accessed | tf_op | source)
XLA Modules:
  0.0 161.8 jit_solution(8054716955889368383)
XLA Ops:
  7.2 0.0 copy-start
  7.2 0.0 copy-start.1
  7.2 0.0 all-reduce.2.cloned.1.call-start
  7.3 0.0 copy-start.2
  7.3 7.3 %fusion = f32[3,6,128,32]{2,3,1,0:T(8,128)S(1)} fusion(f32[3,6,128,512]{3,2,1,0:T(8,128)} %param.5, bf16[3,6,128,512]{3,2,1,0:T(8,128)(2,1)} %param.6, f32[32]{0:T(128)S(1)} %iota_convert_fusion, f32[512]{0:T(512)S(1)} %add_multiply_fusion, f32[32]{0:T(128)S(1)} %compare_select_fusion.1), kind=kOutput, calls=%fused_computation.1 | convolution fusion | flops 455393280 | bytes 7375104 | tf_op jit(solution)/shard_map/...ij,jb->...ib/dot_general | solution.py:27
  14.6 1.2 convolution_bitcast_fusion.1
  15.8 0.0 all-reduce.2.cloned.1.call-update
  15.8 0.0 copy-done
  15.9 0.0 copy-done.1
  15.9 0.3 add_divide_fusion
  16.2 129.9 %all-reduce.2.cloned.1.call-done = f32[3,6,32,32]{2,3,1,0:T(8,128)} async-done(((f32[3,6,32,32]{2,3,1,0:T(8,128)}), f32[3,6,32,32]{2,3,1,0:T(8,128)}) %all-reduce.2.cloned.1.call-update) | async-done | bytes 73744 | tf_op jit(solution)/shard_map/psum | solution.py:28
  146.0 1.1 multiply_reduce_fusion
  147.1 0.6 broadcast_multiply_fusion
  147.7 1.5 convolution_bitcast_fusion
  149.2 0.0 copy-done.2
  149.2 5.8 %multiply_convert_fusion = bf16[3,6,128,512]{3,2,1,0:T(8,128)(2,1)} fusion(f32[3,128,512]{2,1,0:T(8,128)S(1)} %add_divide_fusion, f32[3,6]{1,0:T(4,128)S(1)} %copy-done.2, f32[3,6,128,32]{2,3,1,0:T(8,128)S(1)} %convolution_bitcast_fusion, f32[32]{0:T(128)S(1)} %iota_convert_fusion, f32[512]{0:T(512)S(1)} %add_multiply_fusion, f32[32]{0:T(128)S(1)} %compare_select_fusion.1), kind=kOutput, calls=%fused_computation | convolution fusion | flops 456572928 | bytes 3443016 | tf_op jit(solution)/shard_map/lvib,jb->lvij/dot_general | solution.py:34
  (5 shorter events, 0.0 us)
Async XLA Ops:
  7.2 8.7 %copy-start = (f32[128,512]{1,0:T(8,128)S(1)}, f32[128,512]{1,0:T(8,128)}, u32[]{:S(2)}) copy-start(f32[128,512]{1,0:T(8,128)} %param.9) | copy-start | bytes 786436
  7.2 8.7 %copy-start.1 = (f32[3]{0:T(128)S(1)}, f32[3]{0:T(128)}, u32[]{:S(2)}) copy-start(f32[3]{0:T(128)} %param.8) | copy-start | bytes 40
  7.2 138.9 %all-reduce.2.cloned.1.call-start = ((), (), s32[]{:S(2)}) async-start(), calls=%async_computation | async-start | bytes 589824 | tf_op jit(solution)/shard_map/psum | solution.py:28
  7.3 141.9 %copy-start.2 = (f32[3,6]{1,0:T(4,128)S(1)}, f32[3,6]{1,0:T(4,128)}, u32[]{:S(2)}) copy-start(f32[3,6]{1,0:T(4,128)} %param.7) | copy-start | bytes 220
Sparse Core Ops, SparseCore 0:
  16.0 130.0 all-reduce.1
where the time goes:
time: 162 us
  waiting for transfers between devices  130 us (80%)
  matrix products  15.7 us (10%)
  between operations  14.1 us (9%)
  other arithmetic  2 us (1%)
    psum x1, waiting for transfers between devices, per_device(): lax.psum(jnp.einsum('ia,...ib->...ab', row_table, part, precision=largest...  130 us
    dot_general x1, matrix products, per_device(): jnp.einsum('...ij,jb->...ib', diff, col_table, precision=largest_wavenumber)  7.27 us
    dot_general x1, matrix products, per_device(): jnp.einsum('lvib,jb->lvij', restored_fields, col_table, precision=largest...  5.76 us
  transfers between devices with their start and end apart: 1, of which 1 were waited for; matrix products, arithmetic and copies ran while one was open for 0% of the time, Pallas kernels for 0%

commit v1 on v0

--- a/solution.py
+++ b/solution.py
@@ -25,8 +25,12 @@
     col_table = cosine_table(cols * lax.axis_size("gy"), KY, lax.axis_index("gy") * cols, cols)
     diff = forcing_host_values.astype(jnp.float32) - prognostic_values
     part = jnp.einsum("...ij,jb->...ib", diff, col_table, precision=largest_wavenumber)
-    mode_factors = lax.psum(
-        jnp.einsum("ia,...ib->...ab", row_table, part, precision=largest_wavenumber), ("gx", "gy")
+    mode_factors = jnp.sum(
+        lax.all_gather(
+            jnp.einsum("ia,...ib->...ab", row_table, part, precision=largest_wavenumber),
+            ("gx", "gy"),
+        ),
+        axis=0,
     )
     restored_fields = jnp.einsum(
         "ia,lvab->lvib", row_table, mode_factors, precision=largest_wavenumber

time: 162 us -> 120 us (0.74); the launches traced: 162 us -> 118 us
  waiting for transfers between devices: 130 us -> 82.4 us
  other arithmetic: 2 us -> 5.93 us
    psum x1 -> x0, waiting for transfers between devices: 130 us -> none  [per_device(): lax.psum(jnp.einsum('ia,...ib->...ab', row_table, part, precision=largest...]
    all_gather x0 -> x1, waiting for transfers between devices: none -> 82.3 us  [per_device(): lax.all_gather(jnp.einsum('ia,...ib->...ab', row_table, part, precision=l...]
    unnamed x0 -> x1, other arithmetic: none -> 4.89 us
where the time goes in v1:
time: 120 us; the launch traced here: 118 us
  waiting for transfers between devices  82.4 us (69%)
  matrix products  14.2 us (12%)
  between operations  14.1 us (12%)
  other arithmetic  5.93 us (5%)
    all_gather x1, waiting for transfers between devices, per_device(): lax.all_gather(jnp.einsum('ia,...ib->...ab', row_table, part, precision=l...  82.3 us
    dot_general x1, matrix products, per_device(): jnp.einsum('...ij,jb->...ib', diff, col_table, precision=largest_wavenumber)  7.28 us
    dot_general x1, matrix products, per_device(): jnp.einsum('lvib,jb->lvij', restored_fields, col_table, precision=largest...  5.74 us
    unnamed x1, other arithmetic  4.89 us
  transfers between devices with their start and end apart: 1, of which 1 were waited for; matrix products, arithmetic and copies ran while one was open for 0% of the time, Pallas kernels for 0%

profile of v1, /device:TPU:8, one launch (start us, length us, event | category | flops | bytes accessed | tf_op | source)
XLA Modules:
  0.0 117.7 jit_solution(5494117906103019869)
XLA Ops:
  7.2 0.0 copy-start
  7.2 0.0 copy-start.1
  7.2 0.0 all-gather.3.cloned.1.call-start
  7.3 7.3 %fusion = f32[3,6,128,32]{2,3,1,0:T(8,128)S(1)} fusion(f32[3,6,128,512]{3,2,1,0:T(8,128)} %param.5, bf16[3,6,128,512]{3,2,1,0:T(8,128)(2,1)} %param.6, f32[32]{0:T(128)S(1)} %iota_convert_fusion, f32[512]{0:T(512)S(1)} %add_multiply_fusion, f32[32]{0:T(128)S(1)} %compare_select_fusion.1), kind=kOutput, calls=%fused_computation.1 | convolution fusion | flops 455393280 | bytes 7375104 | tf_op jit(solution)/shard_map/...ij,jb->...ib/dot_general | solution.py:27
  14.6 0.5 convolution_bitcast_fusion.1
  15.1 0.9 copy.7
  16.0 0.0 all-gather.3.cloned.1.call-update
  16.0 0.0 copy-done
  16.0 0.0 copy-done.1
  16.0 0.3 add_divide_fusion
  16.3 82.3 %all-gather.3.cloned.1.call-done = f32[96,6,32,32]{3,2,1,0:T(8,128)} async-done(((f32[3,6,32,32]{3,2,1,0:T(8,128)}), f32[96,6,32,32]{3,2,1,0:T(8,128)}) %all-gather.3.cloned.1.call-update) | async-done | bytes 2359312 | tf_op jit(solution)/shard_map/all_gather | solution.py:29
  98.6 0.0 copy-start.2
  98.6 4.9 %reduce_sum.18 = f32[3,6,32,32]{3,2,1,0:T(8,128)S(1)} reduce(f32[32,3,6,32,32]{4,3,2,1,0:T(8,128)} %bitcast.22, f32[]{:T(128)} %constant.16.clone.1), dimensions={0}, to_apply=%region_0.1 | reduce | flops 571392 | bytes 2433028
  103.5 0.7 convolution_bitcast_fusion
  104.2 0.1 copy.11
  104.4 0.1 multiply_reduce_fusion
  104.5 0.6 broadcast_multiply_fusion
  105.1 0.0 copy-done.2
  105.1 5.7 %multiply_convert_fusion = bf16[3,6,128,512]{3,2,1,0:T(8,128)(2,1)} fusion(f32[3,128,512]{2,1,0:T(8,128)S(1)} %add_divide_fusion, f32[3,6]{1,0:T(4,128)S(1)} %copy-done.2, f32[3,6,128,32]{2,3,1,0:T(8,128)S(1)} %convolution_bitcast_fusion, f32[32]{0:T(128)S(1)} %iota_convert_fusion, f32[512]{0:T(512)S(1)} %add_multiply_fusion, f32[32]{0:T(128)S(1)} %compare_select_fusion.1), kind=kOutput, calls=%fused_computation | convolution fusion | flops 456572928 | bytes 3443016 | tf_op jit(solution)/shard_map/lvib,jb->lvij/dot_general | solution.py:38
  (5 shorter events, 0.0 us)
Async XLA Ops:
  7.2 8.8 %copy-start = (f32[128,512]{1,0:T(8,128)S(1)}, f32[128,512]{1,0:T(8,128)}, u32[]{:S(2)}) copy-start(f32[128,512]{1,0:T(8,128)} %param.9) | copy-start | bytes 786436
  7.2 8.8 %copy-start.1 = (f32[3]{0:T(128)S(1)}, f32[3]{0:T(128)}, u32[]{:S(2)}) copy-start(f32[3]{0:T(128)} %param.8) | copy-start | bytes 40
  7.2 91.5 %all-gather.3.cloned.1.call-start = ((), (), s32[]{:S(2)}) async-start(), calls=%async_computation | async-start | bytes 9732096 | tf_op jit(solution)/shard_map/all_gather | solution.py:29
  98.6 6.4 %copy-start.2 = (f32[3,6]{1,0:T(4,128)S(1)}, f32[3,6]{1,0:T(4,128)}, u32[]{:S(2)}) copy-start(f32[3,6]{1,0:T(4,128)} %param.7) | copy-start | bytes 220
Sparse Core Ops, SparseCore 0:
  16.1 82.4 all-gather.2
